TPU v7x, 512 devices: a whole 4x8x8 slice. The times are simulated.
512 devices in a mesh: gx: 8 (over z), gy: 64 (over x, y, core).
Axes of the slice: x: 4, y: 8, z: 8, core: 2. Of those that a mesh axis runs over, the one named last changes fastest.
Arguments:
- right_side: float32 [4194304], P(('gx', 'gy')), may hold values from -60 to 60
- reaction: float32 [4194304], P(('gx', 'gy')), may hold values from 0.5 to 2
- cell_slots: int32 [125, 65536], P(None, ('gx', 'gy')), may hold values from 0 to 12543
- cell_level: int32 [65536], P(('gx', 'gy')), may hold values from 0 to 2
- con_masters: int32 [5, 131072], P(None, ('gx', 'gy')), may hold values from 0 to 12287
- con_rows: int32 [131072], P(('gx', 'gy')), may hold values from 0 to 9
- send_lists: int32 [8, 262144], P(None, ('gx', 'gy')), may hold values from 0 to 8191
Outputs:
- solution: float32 [4194304], P(('gx', 'gy'))
- residual: float32 [4194304], P(('gx', 'gy'))
Inputs may be any that keep to these rules, and one draw needn't show every extreme that they name: `cell_slots`: column block of rank d indexes d's local list: its 8192 owned unknowns, then 512 values from each of ranks d - 1, ..., d - 4, then from d + 1, ..., d + 4, then its 256 constrained values (rank d = 64 gx + gy). `cell_level`: A cell of level l has side 2^(-l). `con_masters`: slots among the same rank's owned and ghost values. `con_rows`: row of the interpolation table: 5 fine nodes on each half of a coarse edge. `send_lists`: row j of rank s lists s's owned unknowns that fill ghost block j of rank s + j + 1 (j < 4) or of rank s - (j - 3); rows without such a rank are unused.
All inputs are finite; a program needn't handle non-finite values.
Results may differ from a plain program's by a relative error of at most 0.0002.
Values sent between devices are 32-bit elements; how exact they have to be, the bound alone decides.
No kernel may reach another device: no remote copies, remote signals or barrier semaphores. Data moves between devices by JAX's collectives and lax.ppermute only.
A program may use at most 64 MiB of HBM per device.

v0:
```python
import jax
import jax.numpy as jnp
import numpy as np
from jax import lax
from jax.sharding import Mesh
from jax.sharding import PartitionSpec as P

ITERS = 3
GX_GY = ("gx", "gy_0", "gy_1", "gy_2")


def shifted(value, axis, steps):
    count = lax.axis_size(axis)
    initial, last = (max(0, -steps), min(count, count - steps))
    return lax.ppermute(value, axis, [(source, source + steps) for source in range(initial, last)])


def one_axis_at_a_time(x, axes):
    for axis in axes:
        x = lax.psum(x, axis)
    return x


def lagrange(node_list, points):
    node_count = len(node_list)
    values = np.ones((len(points), node_count))
    derivs = np.zeros((len(points), node_count))
    for basis_node in range(node_count):
        for other_node in range(node_count):
            if other_node != basis_node:
                values[:, basis_node] = (
                    values[:, basis_node]
                    * (points - node_list[other_node])
                    / (node_list[basis_node] - node_list[other_node])
                )
        for skipped in range(node_count):
            if skipped != basis_node:
                product_term = np.ones(len(points)) / (node_list[basis_node] - node_list[skipped])
                for other_node in range(node_count):
                    if other_node != basis_node and other_node != skipped:
                        product_term = (
                            product_term
                            * (points - node_list[other_node])
                            / (node_list[basis_node] - node_list[other_node])
                        )
                derivs[:, basis_node] = derivs[:, basis_node] + product_term
    return (values, derivs)


def tables():
    gll_offset = np.sqrt(3.0 / 7.0)
    lobatto = np.array([0.0, (1.0 - gll_offset) / 2.0, 0.5, (1.0 + gll_offset) / 2.0, 1.0])
    inner_point = np.sqrt(5.0 - 2.0 * np.sqrt(10.0 / 7.0)) / 3.0
    outer_point = np.sqrt(5.0 + 2.0 * np.sqrt(10.0 / 7.0)) / 3.0
    inner_weight = (322.0 + 13.0 * np.sqrt(70.0)) / 900.0
    outer_weight = (322.0 - 13.0 * np.sqrt(70.0)) / 900.0
    points = np.array([-outer_point, -inner_point, 0.0, inner_point, outer_point])
    gauss_weights = np.array(
        [outer_weight, inner_weight, 128.0 / 225.0, inner_weight, outer_weight]
    )
    points = (points + 1.0) / 2.0
    gauss_weights = gauss_weights / 2.0
    shapes, slopes = lagrange(lobatto, points)
    fine_points = np.concatenate([lobatto / 2.0, (1.0 + lobatto) / 2.0])
    interp, unused_slopes = lagrange(lobatto, fine_points)
    quad_weights = np.kron(gauss_weights, np.kron(gauss_weights, gauss_weights))
    grad_x = np.kron(slopes, np.kron(shapes, shapes))
    grad_y = np.kron(shapes, np.kron(slopes, shapes))
    grad_z = np.kron(shapes, np.kron(shapes, slopes))
    stiffness = np.zeros((125, 125))
    for gradient in (grad_x, grad_y, grad_z):
        stiffness = stiffness + gradient.T @ (quad_weights[:, None] * gradient)
    return (jnp.asarray(interp, jnp.float32), jnp.asarray(stiffness, jnp.float32))


def cell_laplace(cell_values, cell_scale, stiffness):
    product = jnp.dot(
        stiffness, cell_values, precision=lax.Precision.HIGHEST, preferred_element_type=jnp.float32
    )
    return product * cell_scale[None, :]


def local_apply(own_values, ghosts, slot_map, cell_scale, masters, weights, stiffness):
    local_list = jnp.concatenate([own_values, ghosts.reshape(-1)])
    picked = local_list[masters]
    resolved = jnp.sum(weights * picked, axis=0)
    full_list = jnp.concatenate([local_list, resolved])
    cell_values = full_list[slot_map]
    contrib = cell_laplace(cell_values, cell_scale, stiffness)
    summed = (
        jnp.zeros(full_list.shape, jnp.float32).at[slot_map.reshape(-1)].add(contrib.reshape(-1))
    )
    split_at = local_list.shape[0]
    spread = (
        summed[:split_at]
        .at[masters.reshape(-1)]
        .add((weights * summed[split_at:][None, :]).reshape(-1))
    )
    return spread


def on_device(right_side, reaction, cell_slots, cell_level, con_masters, con_rows, send_lists):
    interp, stiffness = tables()
    block_count = send_lists.shape[0]
    half_count = block_count // 2
    offsets = [neighbour + 1 for neighbour in range(half_count)] + [
        -(neighbour + 1) for neighbour in range(half_count)
    ]
    cell_scale = jnp.exp2(-cell_level.astype(jnp.float32))
    selector = (con_rows[None, :] == jnp.arange(10, dtype=jnp.int32)[:, None]).astype(jnp.float32)
    weights = jnp.dot(interp.T, selector, precision=lax.Precision.HIGHEST)
    own_count = right_side.shape[0]
    flat_lists = send_lists.reshape(-1)

    def carry_out(packed):
        return jnp.stack(
            [
                shifted(packed[neighbour], GX_GY, offsets[neighbour])
                for neighbour in range(block_count)
            ]
        )

    def carry_back(packed):
        return jnp.stack(
            [
                shifted(packed[neighbour], GX_GY, -offsets[neighbour])
                for neighbour in range(block_count)
            ]
        )

    def operate(vector):
        ghosts = carry_out(vector[send_lists])
        spread = local_apply(
            vector, ghosts, cell_slots, cell_scale, con_masters, weights, stiffness
        )
        returned = carry_back(spread[own_count:].reshape(block_count, -1))
        result = spread[:own_count] + reaction * vector
        return result.at[flat_lists].add(returned.reshape(-1))

    def paired_sums(vector, applied):
        return (
            one_axis_at_a_time(jnp.sum(vector * vector), GX_GY),
            one_axis_at_a_time(jnp.sum(vector * applied), GX_GY),
        )

    solution = jnp.zeros_like(right_side)
    residual = right_side
    applied = operate(residual)
    norm_now, product = paired_sums(residual, applied)
    step_size = norm_now / product
    direction = residual
    applied_dir = applied
    for iteration in range(ITERS):
        solution = solution + step_size * direction
        residual = residual - step_size * applied_dir
        if iteration + 1 < ITERS:
            applied = operate(residual)
            norm_next, product = paired_sums(residual, applied)
            beta_ratio = norm_next / norm_now
            step_size = norm_next / (product - beta_ratio * norm_next / step_size)
            direction = residual + beta_ratio * direction
            applied_dir = applied + beta_ratio * applied_dir
            norm_now = norm_next
    return (solution, residual)


def solution(mesh):
    torus = Mesh(mesh.devices.reshape(mesh.shape["gx"], 4, 8, 2), ("gx", "gy_0", "gy_1", "gy_2"))
    placed = (
        P(GX_GY),
        P(GX_GY),
        P(None, GX_GY),
        P(GX_GY),
        P(None, GX_GY),
        P(GX_GY),
        P(None, GX_GY),
    )
    return jax.shard_map(
        on_device, mesh=torus, in_specs=placed, out_specs=(P(GX_GY), P(GX_GY)), check_vma=False
    )
```

profile of v0, /device:TPU:1, one launch (start us, length us, event | category | flops | bytes accessed | tf_op | source)
XLA Modules:
  0.0 1038.3 jit_solution(5382295155196519492)
XLA Ops:
  2.1 23.0 %gather_fusion = f32[4096]{0:T(1024)S(1)} fusion(f32[8192]{0:T(1024)S(1)} %copy-done, s32[4096]{0:T(1024)S(1)} %broadcast_clamp_fusion), kind=kCustom, calls=%fused_computation | custom fusion | bytes 49152 | tf_op jit(solution)/shard_map/gather | solution.py:132
  29.1 8.7 collective-permute-start.4
  37.8 6.4 collective-permute-start.3
  44.6 6.2 collective-permute-start.2
  50.9 3.4 collective-permute-start.1
  54.2 1.9 collective-permute-start
  57.4 7.1 gather_fusion.1
  65.4 82.3 %gather_fusion.2 = f32[16000]{0:T(1024)S(1)} fusion(f32[12544]{0:T(1024)S(1)} %pad_maximum_fusion, s32[16384]{0:T(1024)S(1)} %pad_clamp_fusion), kind=kCustom, calls=%fused_computation.2 | custom fusion | bytes 192000 | tf_op jit(solution)/shard_map/gather | solution.py:88
  148.1 85.1 %scatter_custom_fusion = f32[12544]{0:T(1024)S(1)} fusion(s32[16000]{0:T(1024)S(1)} %fusion.7, f32[16000]{0:T(1024)S(1)} %bitcast.115, f32[]{:T(128)} %constant.8.clone.1), kind=kCustom, calls=%fused_computation.59 | custom fusion | flops 16000 | bytes 50180 | tf_op jit(solution)/shard_map/scatter-add | solution.py:91
  233.3 7.4 scatter_fusion
  240.8 1.8 collective-permute-start.15
  242.6 5.5 collective-permute-start.14
  248.2 1.9 collective-permute-start.13
  250.1 2.5 collective-permute-start.12
  256.5 1.9 collective-permute-start.8
  260.2 1.6 collective-permute-done.8
  261.9 22.5 %scatter_fusion.1 = f32[8192]{0:T(1024)S(1)} fusion(f32[8192]{0:T(1024)S(1)} %slice_add_fusion.2, s32[4096]{0:T(1024)S(1)} %bitcast.101, f32[4096]{0:T(1024)S(1)} %bitcast.112), kind=kCustom, calls=%fused_computation.11 | custom fusion | flops 4096 | bytes 65536 | tf_op jit(solution)/shard_map/scatter-add | solution.py:138
  285.0 32.7 %all-reduce.5 = (f32[]{:T(128)}, f32[]{:T(128)}) all-reduce(f32[]{:T(128)} %get-tuple-element.7, f32[]{:T(128)} %get-tuple-element.6), channel_id=1, replica_groups=mesh['gx'=8,'gy_0'=4,'gy_1'=8,'gy_2'=2] {'gx'}, use_global_device_ids=true, to_apply=%region_1.0 | all-reduce | flops 2 | bytes 16 | tf_op jit(solution)/shard_map/psum | solution.py:20
  317.6 6.6 all-reduce.8
  324.2 16.9 %all-reduce.2 = (f32[]{:T(128)}, f32[]{:T(128)}) all-reduce(f32[]{:T(128)} %get-tuple-element.24, f32[]{:T(128)} %get-tuple-element.25), channel_id=1, replica_groups=mesh['gx'=8,'gy_0'=4,'gy_1'=8,'gy_2'=2] {'gy_1'}, use_global_device_ids=true, to_apply=%region_3.0 | all-reduce | flops 2 | bytes 16 | tf_op jit(solution)/shard_map/psum | solution.py:20
  341.1 10.0 all-reduce.11
  352.4 23.0 %gather_fusion.3 = f32[4096]{0:T(1024)S(1)} fusion(f32[8192]{0:T(1024)S(1)} %multiply_subtract_fusion.2, s32[4096]{0:T(1024)S(1)} %broadcast_clamp_fusion), kind=kCustom, calls=%fused_computation.3 | custom fusion | bytes 49152 | tf_op jit(solution)/shard_map/gather | solution.py:132
  379.4 2.3 collective-permute-start.20
  381.7 6.4 collective-permute-start.19
  388.1 6.2 collective-permute-start.18
  394.3 3.4 collective-permute-start.17
  397.7 2.1 collective-permute-start.16
  400.8 7.1 gather_fusion.4
  408.0 82.3 %gather_fusion.5 = f32[16000]{0:T(1024)S(1)} fusion(f32[12544]{0:T(1024)S(1)} %pad_maximum_fusion.1, s32[16384]{0:T(1024)S(1)} %pad_clamp_fusion), kind=kCustom, calls=%fused_computation.5 | custom fusion | bytes 192000 | tf_op jit(solution)/shard_map/gather | solution.py:88
  490.7 85.1 %scatter_custom_fusion.3 = f32[12544]{0:T(1024)S(1)} fusion(s32[16000]{0:T(1024)S(1)} %fusion.7, f32[16000]{0:T(1024)S(1)} %bitcast.116, f32[]{:T(128)} %constant.8.clone.1), kind=kCustom, calls=%fused_computation.57 | custom fusion | flops 16000 | bytes 50180 | tf_op jit(solution)/shard_map/scatter-add | solution.py:91
  575.9 7.6 scatter_fusion.2
  583.5 1.9 collective-permute-start.31
  585.4 6.2 collective-permute-start.30
  591.6 2.0 collective-permute-start.29
  593.6 2.4 collective-permute-start.28
  599.9 2.0 collective-permute-start.24
  601.9 1.7 collective-permute-done.26
  603.7 1.6 collective-permute-done.24
  605.4 22.5 %scatter_fusion.3 = f32[8192]{0:T(1024)S(1)} fusion(f32[8192]{0:T(1024)S(1)} %slice_add_fusion.1, s32[4096]{0:T(1024)S(1)} %bitcast.102, f32[4096]{0:T(1024)S(1)} %bitcast.113), kind=kCustom, calls=%fused_computation.14 | custom fusion | flops 4096 | bytes 65536 | tf_op jit(solution)/shard_map/scatter-add | solution.py:138
  628.6 25.6 %all-reduce.4 = (f32[]{:T(128)}, f32[]{:T(128)}) all-reduce(f32[]{:T(128)} %get-tuple-element.5, f32[]{:T(128)} %get-tuple-element.4), channel_id=1, replica_groups=mesh['gx'=8,'gy_0'=4,'gy_1'=8,'gy_2'=2] {'gx'}, use_global_device_ids=true, to_apply=%region_15.0 | all-reduce | flops 2 | bytes 16 | tf_op jit(solution)/shard_map/psum | solution.py:20
  654.2 6.7 all-reduce.7
  660.9 20.6 %all-reduce.1 = (f32[]{:T(128)}, f32[]{:T(128)}) all-reduce(f32[]{:T(128)} %get-tuple-element.22, f32[]{:T(128)} %get-tuple-element.23), channel_id=1, replica_groups=mesh['gx'=8,'gy_0'=4,'gy_1'=8,'gy_2'=2] {'gy_1'}, use_global_device_ids=true, to_apply=%region_17.0 | all-reduce | flops 2 | bytes 16 | tf_op jit(solution)/shard_map/psum | solution.py:20
  681.5 9.6 all-reduce.10
  695.7 23.0 %gather_fusion.6 = f32[4096]{0:T(1024)S(1)} fusion(f32[8192]{0:T(1024)S(1)} %multiply_subtract_fusion.1, s32[4096]{0:T(1024)S(1)} %broadcast_clamp_fusion), kind=kCustom, calls=%fused_computation.6 | custom fusion | bytes 49152 | tf_op jit(solution)/shard_map/gather | solution.py:132
  722.6 2.3 collective-permute-start.36
  724.9 6.4 collective-permute-start.35
  731.3 6.2 collective-permute-start.34
  737.6 3.4 collective-permute-start.33
  740.9 2.1 collective-permute-start.32
  744.1 7.1 gather_fusion.7
  751.2 82.3 %gather_fusion.8 = f32[16000]{0:T(1024)S(1)} fusion(f32[12544]{0:T(1024)S(1)} %pad_maximum_fusion.2, s32[16384]{0:T(1024)S(1)} %pad_clamp_fusion), kind=kCustom, calls=%fused_computation.8 | custom fusion | bytes 192000 | tf_op jit(solution)/shard_map/gather | solution.py:88
  833.9 85.1 %scatter_custom_fusion.6 = f32[12544]{0:T(1024)S(1)} fusion(s32[16000]{0:T(1024)S(1)} %fusion.7, f32[16000]{0:T(1024)S(1)} %bitcast.114, f32[]{:T(128)} %constant.8.clone.1), kind=kCustom, calls=%fused_computation.55 | custom fusion | flops 16000 | bytes 50180 | tf_op jit(solution)/shard_map/scatter-add | solution.py:91
  919.1 7.4 scatter_fusion.4
  926.5 1.9 collective-permute-start.47
  928.4 6.2 collective-permute-start.46
  934.6 2.0 collective-permute-start.45
  936.6 2.4 collective-permute-start.44
  942.9 2.0 collective-permute-start.40
  945.0 1.7 collective-permute-done.42
  948.5 22.5 %scatter_fusion.5 = f32[8192]{0:T(1024)S(1)} fusion(f32[8192]{0:T(1024)S(1)} %slice_add_fusion, s32[4096]{0:T(1024)S(1)} %bitcast.103, f32[4096]{0:T(1024)S(1)} %bitcast.111), kind=kCustom, calls=%fused_computation.17 | custom fusion | flops 4096 | bytes 65536 | tf_op jit(solution)/shard_map/scatter-add | solution.py:138
  971.5 25.5 %all-reduce.3 = (f32[]{:T(128)}, f32[]{:T(128)}) all-reduce(f32[]{:T(128)} %get-tuple-element.3, f32[]{:T(128)} %get-tuple-element.2), channel_id=1, replica_groups=mesh['gx'=8,'gy_0'=4,'gy_1'=8,'gy_2'=2] {'gx'}, use_global_device_ids=true, to_apply=%region_29.0 | all-reduce | flops 2 | bytes 16 | tf_op jit(solution)/shard_map/psum | solution.py:20
  997.1 6.6 all-reduce.6
  1003.7 20.0 %all-reduce = (f32[]{:T(128)}, f32[]{:T(128)}) all-reduce(f32[]{:T(128)} %get-tuple-element.20, f32[]{:T(128)} %get-tuple-element.21), channel_id=1, replica_groups=mesh['gx'=8,'gy_0'=4,'gy_1'=8,'gy_2'=2] {'gy_1'}, use_global_device_ids=true, to_apply=%region_31.0 | all-reduce | flops 2 | bytes 16 | tf_op jit(solution)/shard_map/psum | solution.py:20
  1023.6 10.1 all-reduce.9
  (151 shorter events, 36.6 us)
Async XLA Ops:
  1.4 0.8 copy-start
  2.1 42.2 %copy-start.8 = (s32[128]{0:T(128)S(1)}, s32[128]{0:T(128)}, u32[]{:S(2)}) copy-start(s32[128]{0:T(128)} %param.12) | copy-start | bytes 1540
  2.1 42.2 %copy-start.5 = (s32[5,256]{1,0:T(8,128)S(1)}, s32[5,256]{1,0:T(8,128)}, u32[]{:S(2)}) copy-start(s32[5,256]{1,0:T(8,128)} %param.13) | copy-start | bytes 15364
  25.1 19.2 %copy-start.3 = (s32[125,128]{1,0:T(8,128)S(1)}, s32[125,128]{1,0:T(8,128)}, u32[]{:S(2)}) copy-start(s32[125,128]{1,0:T(8,128)} %param.11) | copy-start | bytes 192004
  25.2 19.5 %collective-permute-start.7 = (f32[512]{0:T(512)S(1)}, f32[512]{0:T(512)S(1)}, u32[]{:S(2)}, u32[]{:S(2)}) collective-permute-start(f32[512]{0:T(512)S(1)} %get-tuple-element.74), channel_id=1, source_target_pairs={{4,0},{5,1},{6,2},{7,3},{8,4},{9,5},{10,6},{11,7},{12,8},{13,9},{1... | collective-permute-start | bytes 6152 | tf_op jit(solution)/shard_map/ppermute | solution.py:15
  26.5 24.4 %collective-permute-start.6 = (f32[512]{0:T(512)S(1)}, f32[512]{0:T(512)S(1)}, u32[]{:S(2)}, u32[]{:S(2)}) collective-permute-start(f32[512]{0:T(512)S(1)} %get-tuple-element.75), channel_id=1, source_target_pairs={{3,0},{4,1},{5,2},{6,3},{7,4},{8,5},{9,6},{10,7},{11,8},{12,9},{13... | collective-permute-start | bytes 6152 | tf_op jit(solution)/shard_map/ppermute | solution.py:15
  27.8 26.5 %collective-permute-start.5 = (f32[512]{0:T(512)S(1)}, f32[512]{0:T(512)S(1)}, u32[]{:S(2)}, u32[]{:S(2)}) collective-permute-start(f32[512]{0:T(512)S(1)} %get-tuple-element.76), channel_id=1, source_target_pairs={{2,0},{3,1},{4,2},{5,3},{6,4},{7,5},{8,6},{9,7},{10,8},{11,9},{12,... | collective-permute-start | bytes 6152 | tf_op jit(solution)/shard_map/ppermute | solution.py:15
  29.1 27.1 %collective-permute-start.4 = (f32[512]{0:T(512)S(1)}, f32[512]{0:T(512)S(1)}, u32[]{:S(2)}, u32[]{:S(2)}) collective-permute-start(f32[512]{0:T(512)S(1)} %get-tuple-element.77), channel_id=1, source_target_pairs={{1,0},{2,1},{3,2},{4,3},{5,4},{6,5},{7,6},{8,7},{9,8},{10,9},{11,1... | collective-permute-start | bytes 6152 | tf_op jit(solution)/shard_map/ppermute | solution.py:15
  37.8 18.4 %collective-permute-start.3 = (f32[512]{0:T(512)S(1)}, f32[512]{0:T(512)S(1)}, u32[]{:S(2)}, u32[]{:S(2)}) collective-permute-start(f32[512]{0:T(512)S(1)} %get-tuple-element.78), channel_id=1, source_target_pairs={{0,4},{1,5},{2,6},{3,7},{4,8},{5,9},{6,10},{7,11},{8,12},{9,13},{1... | collective-permute-start | bytes 6152 | tf_op jit(solution)/shard_map/ppermute | solution.py:15
  44.6 11.6 %copy-start.4 = (s32[8,512]{1,0:T(8,128)S(1)}, s32[8,512]{1,0:T(8,128)}, u32[]{:S(2)}) copy-start(s32[8,512]{1,0:T(8,128)} %param.15) | copy-start | bytes 49156
  44.6 11.6 %collective-permute-start.2 = (f32[512]{0:T(512)S(1)}, f32[512]{0:T(512)S(1)}, u32[]{:S(2)}, u32[]{:S(2)}) collective-permute-start(f32[512]{0:T(512)S(1)} %get-tuple-element.79), channel_id=1, source_target_pairs={{0,3},{1,4},{2,5},{3,6},{4,7},{5,8},{6,9},{7,10},{8,11},{9,12},{10... | collective-permute-start | bytes 6152 | tf_op jit(solution)/shard_map/ppermute | solution.py:15
  50.9 5.4 collective-permute-start.1
  54.2 3.1 collective-permute-start
  64.4 0.7 copy-start.6
  64.5 0.7 copy-start.7
  65.4 82.4 %copy-start.1 = (f32[125,125]{1,0:T(8,128)S(1)}, f32[125,125]{1,0:T(8,128)}, u32[]{:S(2)}) copy-start(f32[125,125]{1,0:T(8,128)} %constant.15.clone) | copy-start | bytes 187504
  240.8 17.7 %copy-start.2 = (f32[8192]{0:T(1024)S(1)}, f32[8192]{0:T(1024)}, u32[]{:S(2)}) copy-start(f32[8192]{0:T(1024)} %param.10) | copy-start | bytes 98308
  240.8 13.1 %collective-permute-start.15 = (f32[512]{0:T(512)S(1)}, f32[512]{0:T(512)S(1)}, u32[]{:S(2)}, u32[]{:S(2)}) collective-permute-start(f32[512]{0:T(512)S(1)} %get-tuple-element.48), channel_id=1, source_target_pairs={{0,4},{1,5},{2,6},{3,7},{4,8},{5,9},{6,10},{7,11},{8,12},{9,13},{1... | collective-permute-start | bytes 6152 | tf_op jit(solution)/shard_map/ppermute | solution.py:15
  242.6 12.6 %collective-permute-start.14 = (f32[512]{0:T(512)S(1)}, f32[512]{0:T(512)S(1)}, u32[]{:S(2)}, u32[]{:S(2)}) collective-permute-start(f32[512]{0:T(512)S(1)} %get-tuple-element.49), channel_id=1, source_target_pairs={{0,3},{1,4},{2,5},{3,6},{4,7},{5,8},{6,9},{7,10},{8,11},{9,12},{10... | collective-permute-start | bytes 6152 | tf_op jit(solution)/shard_map/ppermute | solution.py:15
  248.2 8.4 collective-permute-start.13
  250.1 8.4 collective-permute-start.12
  252.6 5.9 collective-permute-start.11
  253.9 6.2 collective-permute-start.10
  255.2 5.0 collective-permute-start.9
  256.5 5.3 collective-permute-start.8
  375.5 12.6 %collective-permute-start.23 = (f32[512]{0:T(512)S(1)}, f32[512]{0:T(512)S(1)}, u32[]{:S(2)}, u32[]{:S(2)}) collective-permute-start(f32[512]{0:T(512)S(1)} %get-tuple-element.66), channel_id=1, source_target_pairs={{4,0},{5,1},{6,2},{7,3},{8,4},{9,5},{10,6},{11,7},{12,8},{13,9},{1... | collective-permute-start | bytes 6152 | tf_op jit(solution)/shard_map/ppermute | solution.py:15
  376.8 17.5 %collective-permute-start.22 = (f32[512]{0:T(512)S(1)}, f32[512]{0:T(512)S(1)}, u32[]{:S(2)}, u32[]{:S(2)}) collective-permute-start(f32[512]{0:T(512)S(1)} %get-tuple-element.67), channel_id=1, source_target_pairs={{3,0},{4,1},{5,2},{6,3},{7,4},{8,5},{9,6},{10,7},{11,8},{12,9},{13... | collective-permute-start | bytes 6152 | tf_op jit(solution)/shard_map/ppermute | solution.py:15
  378.1 19.6 %collective-permute-start.21 = (f32[512]{0:T(512)S(1)}, f32[512]{0:T(512)S(1)}, u32[]{:S(2)}, u32[]{:S(2)}) collective-permute-start(f32[512]{0:T(512)S(1)} %get-tuple-element.68), channel_id=1, source_target_pairs={{2,0},{3,1},{4,2},{5,3},{6,4},{7,5},{8,6},{9,7},{10,8},{11,9},{12,... | collective-permute-start | bytes 6152 | tf_op jit(solution)/shard_map/ppermute | solution.py:15
  379.4 20.4 %collective-permute-start.20 = (f32[512]{0:T(512)S(1)}, f32[512]{0:T(512)S(1)}, u32[]{:S(2)}, u32[]{:S(2)}) collective-permute-start(f32[512]{0:T(512)S(1)} %get-tuple-element.69), channel_id=1, source_target_pairs={{1,0},{2,1},{3,2},{4,3},{5,4},{6,5},{7,6},{8,7},{9,8},{10,9},{11,1... | collective-permute-start | bytes 6152 | tf_op jit(solution)/shard_map/ppermute | solution.py:15
  381.7 18.1 %collective-permute-start.19 = (f32[512]{0:T(512)S(1)}, f32[512]{0:T(512)S(1)}, u32[]{:S(2)}, u32[]{:S(2)}) collective-permute-start(f32[512]{0:T(512)S(1)} %get-tuple-element.70), channel_id=1, source_target_pairs={{0,4},{1,5},{2,6},{3,7},{4,8},{5,9},{6,10},{7,11},{8,12},{9,13},{1... | collective-permute-start | bytes 6152 | tf_op jit(solution)/shard_map/ppermute | solution.py:15
  388.1 11.7 %collective-permute-start.18 = (f32[512]{0:T(512)S(1)}, f32[512]{0:T(512)S(1)}, u32[]{:S(2)}, u32[]{:S(2)}) collective-permute-start(f32[512]{0:T(512)S(1)} %get-tuple-element.71), channel_id=1, source_target_pairs={{0,3},{1,4},{2,5},{3,6},{4,7},{5,8},{6,9},{7,10},{8,11},{9,12},{10... | collective-permute-start | bytes 6152 | tf_op jit(solution)/shard_map/ppermute | solution.py:15
  394.3 5.5 collective-permute-start.17
  397.7 3.1 collective-permute-start.16
  583.5 13.8 %collective-permute-start.31 = (f32[512]{0:T(512)S(1)}, f32[512]{0:T(512)S(1)}, u32[]{:S(2)}, u32[]{:S(2)}) collective-permute-start(f32[512]{0:T(512)S(1)} %get-tuple-element.40), channel_id=1, source_target_pairs={{0,4},{1,5},{2,6},{3,7},{4,8},{5,9},{6,10},{7,11},{8,12},{9,13},{1... | collective-permute-start | bytes 6152 | tf_op jit(solution)/shard_map/ppermute | solution.py:15
  585.4 13.2 %collective-permute-start.30 = (f32[512]{0:T(512)S(1)}, f32[512]{0:T(512)S(1)}, u32[]{:S(2)}, u32[]{:S(2)}) collective-permute-start(f32[512]{0:T(512)S(1)} %get-tuple-element.41), channel_id=1, source_target_pairs={{0,3},{1,4},{2,5},{3,6},{4,7},{5,8},{6,9},{7,10},{8,11},{9,12},{10... | collective-permute-start | bytes 6152 | tf_op jit(solution)/shard_map/ppermute | solution.py:15
  591.6 8.3 collective-permute-start.29
  593.6 8.3 collective-permute-start.28
  596.0 5.9 collective-permute-start.27
  597.3 6.4 collective-permute-start.26
  598.6 5.1 collective-permute-start.25
  599.9 5.5 collective-permute-start.24
  718.7 12.6 %collective-permute-start.39 = (f32[512]{0:T(512)S(1)}, f32[512]{0:T(512)S(1)}, u32[]{:S(2)}, u32[]{:S(2)}) collective-permute-start(f32[512]{0:T(512)S(1)} %get-tuple-element.58), channel_id=1, source_target_pairs={{4,0},{5,1},{6,2},{7,3},{8,4},{9,5},{10,6},{11,7},{12,8},{13,9},{1... | collective-permute-start | bytes 6152 | tf_op jit(solution)/shard_map/ppermute | solution.py:15
  720.0 17.5 %collective-permute-start.38 = (f32[512]{0:T(512)S(1)}, f32[512]{0:T(512)S(1)}, u32[]{:S(2)}, u32[]{:S(2)}) collective-permute-start(f32[512]{0:T(512)S(1)} %get-tuple-element.59), channel_id=1, source_target_pairs={{3,0},{4,1},{5,2},{6,3},{7,4},{8,5},{9,6},{10,7},{11,8},{12,9},{13... | collective-permute-start | bytes 6152 | tf_op jit(solution)/shard_map/ppermute | solution.py:15
  721.3 19.6 %collective-permute-start.37 = (f32[512]{0:T(512)S(1)}, f32[512]{0:T(512)S(1)}, u32[]{:S(2)}, u32[]{:S(2)}) collective-permute-start(f32[512]{0:T(512)S(1)} %get-tuple-element.60), channel_id=1, source_target_pairs={{2,0},{3,1},{4,2},{5,3},{6,4},{7,5},{8,6},{9,7},{10,8},{11,9},{12,... | collective-permute-start | bytes 6152 | tf_op jit(solution)/shard_map/ppermute | solution.py:15
  722.6 20.4 %collective-permute-start.36 = (f32[512]{0:T(512)S(1)}, f32[512]{0:T(512)S(1)}, u32[]{:S(2)}, u32[]{:S(2)}) collective-permute-start(f32[512]{0:T(512)S(1)} %get-tuple-element.61), channel_id=1, source_target_pairs={{1,0},{2,1},{3,2},{4,3},{5,4},{6,5},{7,6},{8,7},{9,8},{10,9},{11,1... | collective-permute-start | bytes 6152 | tf_op jit(solution)/shard_map/ppermute | solution.py:15
  724.9 18.1 %collective-permute-start.35 = (f32[512]{0:T(512)S(1)}, f32[512]{0:T(512)S(1)}, u32[]{:S(2)}, u32[]{:S(2)}) collective-permute-start(f32[512]{0:T(512)S(1)} %get-tuple-element.62), channel_id=1, source_target_pairs={{0,4},{1,5},{2,6},{3,7},{4,8},{5,9},{6,10},{7,11},{8,12},{9,13},{1... | collective-permute-start | bytes 6152 | tf_op jit(solution)/shard_map/ppermute | solution.py:15
  731.3 11.7 %collective-permute-start.34 = (f32[512]{0:T(512)S(1)}, f32[512]{0:T(512)S(1)}, u32[]{:S(2)}, u32[]{:S(2)}) collective-permute-start(f32[512]{0:T(512)S(1)} %get-tuple-element.63), channel_id=1, source_target_pairs={{0,3},{1,4},{2,5},{3,6},{4,7},{5,8},{6,9},{7,10},{8,11},{9,12},{10... | collective-permute-start | bytes 6152 | tf_op jit(solution)/shard_map/ppermute | solution.py:15
  737.6 5.5 collective-permute-start.33
  740.9 3.1 collective-permute-start.32
  926.5 13.8 %collective-permute-start.47 = (f32[512]{0:T(512)S(1)}, f32[512]{0:T(512)S(1)}, u32[]{:S(2)}, u32[]{:S(2)}) collective-permute-start(f32[512]{0:T(512)S(1)} %get-tuple-element.32), channel_id=1, source_target_pairs={{0,4},{1,5},{2,6},{3,7},{4,8},{5,9},{6,10},{7,11},{8,12},{9,13},{1... | collective-permute-start | bytes 6152 | tf_op jit(solution)/shard_map/ppermute | solution.py:15
  928.4 13.2 %collective-permute-start.46 = (f32[512]{0:T(512)S(1)}, f32[512]{0:T(512)S(1)}, u32[]{:S(2)}, u32[]{:S(2)}) collective-permute-start(f32[512]{0:T(512)S(1)} %get-tuple-element.33), channel_id=1, source_target_pairs={{0,3},{1,4},{2,5},{3,6},{4,7},{5,8},{6,9},{7,10},{8,11},{9,12},{10... | collective-permute-start | bytes 6152 | tf_op jit(solution)/shard_map/ppermute | solution.py:15
  934.6 8.3 collective-permute-start.45
  936.6 8.3 collective-permute-start.44
  939.0 5.9 collective-permute-start.43
  940.3 6.4 collective-permute-start.42
  941.6 5.1 collective-permute-start.41
  942.9 5.5 collective-permute-start.40
where the time goes:
time: 1040 us
  other arithmetic  349 us (34%)
  local copies, waits for them, and re-layouts  339 us (33%)
  blocking collectives  191 us (18%)
  starting transfers between devices  133 us (13%)
  waiting for transfers between devices  13.3 us (1%)
  between operations  11.8 us (1%)
    scatter-add x3, other arithmetic, local_apply(): jnp.zeros(full_list.shape, jnp.float32).at[slot_map.reshape(-1)]  255 us
    gather x3, local copies, waits for them, and re-layouts, local_apply(): cell_values = full_list[slot_map]  247 us
    psum x12, blocking collectives, one_axis_at_a_time(): x = lax.psum(x, axis)  191 us
    ppermute x48, starting transfers between devices, shifted(): lax.ppermute(value, axis, [(source, source + steps) for source in range(i...  133 us
    gather x3, local copies, waits for them, and re-layouts, operate(): ghosts = carry_out(vector[send_lists])  69.1 us
    scatter-add x3, other arithmetic, operate(): return result.at[flat_lists].add(returned.reshape(-1))  67.4 us
    scatter-add x3, other arithmetic, local_apply(): spread = summed[:split_at].at[masters.reshape(-1)].add((weights * summed[...  22.4 us
    gather x6, local copies, waits for them, and re-layouts, local_apply(): picked = local_list[masters]  21.3 us
  transfers between devices with their start and end apart: 48, of which 12 were waited for; matrix products, arithmetic and copies ran while one was open for 0% of the time, Pallas kernels for 0%

commit v1 on v0

--- a/solution.py
+++ b/solution.py
@@ -17,7 +17,7 @@
 
 def one_axis_at_a_time(x, axes):
     for axis in axes:
-        x = lax.psum(x, axis)
+        x = jnp.sum(lax.all_gather(x, axis), axis=0)
     return x
 
 

time: 1040 us -> 1090 us (1.048)
  local copies, waits for them, and re-layouts: 339 us -> 378 us
  other arithmetic: 349 us -> 364 us
  blocking collectives: 191 us -> 178 us
    psum x12 -> x0, blocking collectives: 191 us -> none  [one_axis_at_a_time(): x = lax.psum(x, axis)]
    unnamed x0 -> x12, blocking collectives: none -> 178 us
    unnamed x27 -> x79, local copies, waits for them, and re-layouts: 1.53 us -> 40.2 us
    reduce_sum x0 -> x24, other arithmetic: none -> 14.8 us  [one_axis_at_a_time(): x = jnp.sum(lax.all_gather(x, axis), axis=0)]
  transfers between devices with their start and end apart: 48 -> 48, of which waited for: 12 -> 10; matrix products, arithmetic and copies ran while one was open for 0% -> 0% of each run, Pallas kernels for 0% -> 0%
where the time goes in v1:
time: 1090 us
  local copies, waits for them, and re-layouts  378 us (35%)
  other arithmetic  364 us (33%)
  blocking collectives  178 us (16%)
  starting transfers between devices  141 us (13%)
  waiting for transfers between devices  12.6 us (1%)
  between operations  11.7 us (1%)
    scatter-add x3, other arithmetic, local_apply(): jnp.zeros(full_list.shape, jnp.float32).at[slot_map.reshape(-1)]  255 us
    gather x3, local copies, waits for them, and re-layouts, local_apply(): cell_values = full_list[slot_map]  247 us
    unnamed x12, blocking collectives  178 us
    ppermute x48, starting transfers between devices, shifted(): lax.ppermute(value, axis, [(source, source + steps) for source in range(i...  141 us
    gather x3, local copies, waits for them, and re-layouts, operate(): ghosts = carry_out(vector[send_lists])  69.1 us
    scatter-add x3, other arithmetic, operate(): return result.at[flat_lists].add(returned.reshape(-1))  67.4 us
    unnamed x79, local copies, waits for them, and re-layouts  40.2 us
    scatter-add x3, other arithmetic, local_apply(): spread = summed[:split_at].at[masters.reshape(-1)].add((weights * summed[...  22.5 us
  transfers between devices with their start and end apart: 48, of which 10 were waited for; matrix products, arithmetic and copies ran while one was open for 0% of the time, Pallas kernels for 0%

profile of v1, /device:TPU:1, one launch (start us, length us, event | category | flops | bytes accessed | tf_op | source)
XLA Modules:
  0.0 1085.9 jit_solution(9137621864166917298)
XLA Ops:
  2.1 23.0 %gather_fusion = f32[4096]{0:T(1024)S(1)} fusion(f32[8192]{0:T(1024)S(1)} %copy-done, s32[4096]{0:T(1024)S(1)} %broadcast_clamp_fusion), kind=kCustom, calls=%fused_computation | custom fusion | bytes 49152 | tf_op jit(solution)/shard_map/gather | solution.py:132
  25.2 5.6 collective-permute-start.2
  30.8 5.4 collective-permute-start.3
  36.2 1.9 collective-permute-start.4
  43.0 4.3 collective-permute-start
  47.3 4.9 collective-permute-start.1
  53.0 7.1 gather_fusion.1
  61.1 82.3 %gather_fusion.2 = f32[16000]{0:T(1024)S(1)} fusion(f32[12544]{0:T(1024)S(1)} %pad_maximum_fusion, s32[16384]{0:T(1024)S(1)} %pad_clamp_fusion), kind=kCustom, calls=%fused_computation.2 | custom fusion | bytes 192000 | tf_op jit(solution)/shard_map/gather | solution.py:88
  143.8 85.1 %scatter_custom_fusion = f32[12544]{0:T(1024)S(1)} fusion(s32[16000]{0:T(1024)S(1)} %fusion.7, f32[16000]{0:T(1024)S(1)} %bitcast.143, f32[]{:T(128)} %constant.8.clone.1), kind=kCustom, calls=%fused_computation.59 | custom fusion | flops 16000 | bytes 50180 | tf_op jit(solution)/shard_map/scatter-add | solution.py:91
  229.0 7.4 scatter_fusion
  236.4 1.9 collective-permute-start.8
  243.6 4.3 collective-permute-start.12
  247.9 4.9 collective-permute-start.13
  252.8 4.7 collective-permute-start.14
  257.5 6.1 collective-permute-start.15
  264.3 22.5 %scatter_fusion.1 = f32[8192]{0:T(1024)S(1)} fusion(f32[8192]{0:T(1024)S(1)} %slice_add_fusion.2, s32[4096]{0:T(1024)S(1)} %bitcast.129, f32[4096]{0:T(1024)S(1)} %bitcast.140), kind=kCustom, calls=%fused_computation.11 | custom fusion | flops 4096 | bytes 65536 | tf_op jit(solution)/shard_map/scatter-add | solution.py:138
  288.9 1.4 dynamic-update-slice.4
  291.6 30.8 %all-reduce.29 = (f32[8]{0:T(128)S(1)}, f32[8]{0:T(128)S(1)}) all-reduce(f32[8]{0:T(128)S(1)} %dynamic-update-slice, f32[8]{0:T(128)S(1)} %dynamic-update-slice.4), channel_id=1, replica_groups=mesh['gx'=8,'gy_0'=4,'gy_1'=8,'gy_2'=2] {'gx'}, use_global_device_ids=true, to_apply=%add | all-reduce | flops 16 | bytes 128
  327.6 6.0 all-reduce.32
  338.7 13.4 %all-reduce.26 = (f32[8]{0:T(128)S(1)}, f32[8]{0:T(128)S(1)}) all-reduce(f32[8]{0:T(128)S(1)} %dynamic-update-slice.2, f32[8]{0:T(128)S(1)} %dynamic-update-slice.6), channel_id=1, replica_groups=mesh['gx'=8,'gy_0'=4,'gy_1'=8,'gy_2'=2] {'gy_1'}, use_global_device_ids=true, to_apply=%add.2 | all-reduce | flops 16 | bytes 128
  356.1 12.6 %all-reduce.35 = (f32[2]{0:T(128)S(1)}, f32[2]{0:T(128)S(1)}) all-reduce(f32[2]{0:T(128)S(1)} %dynamic-update-slice.3, f32[2]{0:T(128)S(1)} %dynamic-update-slice.7), channel_id=1, replica_groups=mesh['gx'=8,'gy_0'=4,'gy_1'=8,'gy_2'=2] {'gy_2'}, use_global_device_ids=true, to_apply=%add.3 | all-reduce | flops 4 | bytes 32
  371.3 23.0 %gather_fusion.3 = f32[4096]{0:T(1024)S(1)} fusion(f32[8192]{0:T(1024)S(1)} %multiply_subtract_fusion.2, s32[4096]{0:T(1024)S(1)} %broadcast_clamp_fusion), kind=kCustom, calls=%fused_computation.3 | custom fusion | bytes 49152 | tf_op jit(solution)/shard_map/gather | solution.py:132
  394.4 1.9 collective-permute-start.16
  396.3 2.4 collective-permute-start.17
  398.7 1.8 collective-permute-start.18
  400.5 4.4 collective-permute-start.19
  404.9 2.6 collective-permute-start.20
  410.2 1.5 collective-permute-start.23
  412.1 3.1 collective-permute-done.22
  416.6 7.1 gather_fusion.4
  423.7 82.3 %gather_fusion.5 = f32[16000]{0:T(1024)S(1)} fusion(f32[12544]{0:T(1024)S(1)} %pad_maximum_fusion.1, s32[16384]{0:T(1024)S(1)} %pad_clamp_fusion), kind=kCustom, calls=%fused_computation.5 | custom fusion | bytes 192000 | tf_op jit(solution)/shard_map/gather | solution.py:88
  506.5 85.1 %scatter_custom_fusion.3 = f32[12544]{0:T(1024)S(1)} fusion(s32[16000]{0:T(1024)S(1)} %fusion.7, f32[16000]{0:T(1024)S(1)} %bitcast.144, f32[]{:T(128)} %constant.8.clone.1), kind=kCustom, calls=%fused_computation.57 | custom fusion | flops 16000 | bytes 50180 | tf_op jit(solution)/shard_map/scatter-add | solution.py:91
  591.7 7.4 scatter_fusion.2
  599.1 3.2 collective-permute-start.24
  606.2 5.1 collective-permute-start.28
  611.3 6.1 collective-permute-start.29
  617.4 3.9 collective-permute-start.30
  621.3 5.8 collective-permute-start.31
  627.9 22.5 %scatter_fusion.3 = f32[8192]{0:T(1024)S(1)} fusion(f32[8192]{0:T(1024)S(1)} %slice_add_fusion.1, s32[4096]{0:T(1024)S(1)} %bitcast.130, f32[4096]{0:T(1024)S(1)} %bitcast.141), kind=kCustom, calls=%fused_computation.14 | custom fusion | flops 4096 | bytes 65536 | tf_op jit(solution)/shard_map/scatter-add | solution.py:138
  653.8 25.2 %all-reduce.28 = (f32[8]{0:T(128)S(1)}, f32[8]{0:T(128)S(1)}) all-reduce(f32[8]{0:T(128)S(1)} %dynamic-update-slice.8, f32[8]{0:T(128)S(1)} %dynamic-update-slice.12), channel_id=1, replica_groups=mesh['gx'=8,'gy_0'=4,'gy_1'=8,'gy_2'=2] {'gx'}, use_global_device_ids=true, to_apply=%add.8 | all-reduce | flops 16 | bytes 128
  683.0 6.0 all-reduce.31
  692.8 11.5 %all-reduce.25 = (f32[8]{0:T(128)S(1)}, f32[8]{0:T(128)S(1)}) all-reduce(f32[8]{0:T(128)S(1)} %dynamic-update-slice.10, f32[8]{0:T(128)S(1)} %dynamic-update-slice.14), channel_id=1, replica_groups=mesh['gx'=8,'gy_0'=4,'gy_1'=8,'gy_2'=2] {'gy_1'}, use_global_device_ids=true, to_apply=%add.10 | all-reduce | flops 16 | bytes 128
  708.3 12.9 %all-reduce.34 = (f32[2]{0:T(128)S(1)}, f32[2]{0:T(128)S(1)}) all-reduce(f32[2]{0:T(128)S(1)} %dynamic-update-slice.11, f32[2]{0:T(128)S(1)} %dynamic-update-slice.15), channel_id=1, replica_groups=mesh['gx'=8,'gy_0'=4,'gy_1'=8,'gy_2'=2] {'gy_2'}, use_global_device_ids=true, to_apply=%add.11 | all-reduce | flops 4 | bytes 32
  726.9 23.0 %gather_fusion.6 = f32[4096]{0:T(1024)S(1)} fusion(f32[8192]{0:T(1024)S(1)} %multiply_subtract_fusion.1, s32[4096]{0:T(1024)S(1)} %broadcast_clamp_fusion), kind=kCustom, calls=%fused_computation.6 | custom fusion | bytes 49152 | tf_op jit(solution)/shard_map/gather | solution.py:132
  750.0 2.5 collective-permute-start.32
  752.5 1.8 collective-permute-start.33
  754.3 2.4 collective-permute-start.34
  756.7 3.6 collective-permute-start.35
  760.3 2.6 collective-permute-start.36
  767.4 3.1 collective-permute-done.38
  771.9 7.1 gather_fusion.7
  779.1 82.3 %gather_fusion.8 = f32[16000]{0:T(1024)S(1)} fusion(f32[12544]{0:T(1024)S(1)} %pad_maximum_fusion.2, s32[16384]{0:T(1024)S(1)} %pad_clamp_fusion), kind=kCustom, calls=%fused_computation.8 | custom fusion | bytes 192000 | tf_op jit(solution)/shard_map/gather | solution.py:88
  861.8 85.1 %scatter_custom_fusion.6 = f32[12544]{0:T(1024)S(1)} fusion(s32[16000]{0:T(1024)S(1)} %fusion.7, f32[16000]{0:T(1024)S(1)} %bitcast.142, f32[]{:T(128)} %constant.8.clone.1), kind=kCustom, calls=%fused_computation.55 | custom fusion | flops 16000 | bytes 50180 | tf_op jit(solution)/shard_map/scatter-add | solution.py:91
  947.0 7.6 scatter_fusion.4
  954.7 3.2 collective-permute-start.40
  961.7 4.2 collective-permute-start.44
  966.0 6.1 collective-permute-start.45
  972.1 3.9 collective-permute-start.46
  976.0 5.8 collective-permute-start.47
  982.6 22.5 %scatter_fusion.5 = f32[8192]{0:T(1024)S(1)} fusion(f32[8192]{0:T(1024)S(1)} %slice_add_fusion, s32[4096]{0:T(1024)S(1)} %bitcast.131, f32[4096]{0:T(1024)S(1)} %bitcast.139), kind=kCustom, calls=%fused_computation.17 | custom fusion | flops 4096 | bytes 65536 | tf_op jit(solution)/shard_map/scatter-add | solution.py:138
  1008.6 29.5 %all-reduce.27 = (f32[8]{0:T(128)S(1)}, f32[8]{0:T(128)S(1)}) all-reduce(f32[8]{0:T(128)S(1)} %dynamic-update-slice.16, f32[8]{0:T(128)S(1)} %dynamic-update-slice.20), channel_id=1, replica_groups=mesh['gx'=8,'gy_0'=4,'gy_1'=8,'gy_2'=2] {'gx'}, use_global_device_ids=true, to_apply=%add.16 | all-reduce | flops 16 | bytes 128
  1042.1 6.0 all-reduce.30
  1051.9 11.4 %all-reduce.24 = (f32[8]{0:T(128)S(1)}, f32[8]{0:T(128)S(1)}) all-reduce(f32[8]{0:T(128)S(1)} %dynamic-update-slice.18, f32[8]{0:T(128)S(1)} %dynamic-update-slice.22), channel_id=1, replica_groups=mesh['gx'=8,'gy_0'=4,'gy_1'=8,'gy_2'=2] {'gy_1'}, use_global_device_ids=true, to_apply=%add.18 | all-reduce | flops 16 | bytes 128
  1067.2 12.9 %all-reduce.33 = (f32[2]{0:T(128)S(1)}, f32[2]{0:T(128)S(1)}) all-reduce(f32[2]{0:T(128)S(1)} %dynamic-update-slice.19, f32[2]{0:T(128)S(1)} %dynamic-update-slice.23), channel_id=1, replica_groups=mesh['gx'=8,'gy_0'=4,'gy_1'=8,'gy_2'=2] {'gy_2'}, use_global_device_ids=true, to_apply=%add.19 | all-reduce | flops 4 | bytes 32
  (227 shorter events, 87.3 us)
Async XLA Ops:
  1.4 0.8 copy-start
  2.1 38.6 %copy-start.3 = (s32[125,128]{1,0:T(8,128)S(1)}, s32[125,128]{1,0:T(8,128)}, u32[]{:S(2)}) copy-start(s32[125,128]{1,0:T(8,128)} %param.11) | copy-start | bytes 192004
  25.2 15.6 %copy-start.5 = (s32[5,256]{1,0:T(8,128)S(1)}, s32[5,256]{1,0:T(8,128)}, u32[]{:S(2)}) copy-start(s32[5,256]{1,0:T(8,128)} %param.13) | copy-start | bytes 15364
  25.2 16.6 %collective-permute-start.2 = (f32[512]{0:T(512)S(1)}, f32[512]{0:T(512)S(1)}, u32[]{:S(2)}, u32[]{:S(2)}) collective-permute-start(f32[512]{0:T(512)S(1)} %get-tuple-element.79), channel_id=1, source_target_pairs={{0,3},{1,4},{2,5},{3,6},{4,7},{5,8},{6,9},{7,10},{8,11},{9,12},{10... | collective-permute-start | bytes 6152 | tf_op jit(solution)/shard_map/ppermute | solution.py:15
  30.8 12.3 %collective-permute-start.3 = (f32[512]{0:T(512)S(1)}, f32[512]{0:T(512)S(1)}, u32[]{:S(2)}, u32[]{:S(2)}) collective-permute-start(f32[512]{0:T(512)S(1)} %get-tuple-element.78), channel_id=1, source_target_pairs={{0,4},{1,5},{2,6},{3,7},{4,8},{5,9},{6,10},{7,11},{8,12},{9,13},{1... | collective-permute-start | bytes 6152 | tf_op jit(solution)/shard_map/ppermute | solution.py:15
  36.2 11.1 %collective-permute-start.4 = (f32[512]{0:T(512)S(1)}, f32[512]{0:T(512)S(1)}, u32[]{:S(2)}, u32[]{:S(2)}) collective-permute-start(f32[512]{0:T(512)S(1)} %get-tuple-element.77), channel_id=1, source_target_pairs={{1,0},{2,1},{3,2},{4,3},{5,4},{6,5},{7,6},{8,7},{9,8},{10,9},{11,1... | collective-permute-start | bytes 6152 | tf_op jit(solution)/shard_map/ppermute | solution.py:15
  38.1 14.2 %collective-permute-start.5 = (f32[512]{0:T(512)S(1)}, f32[512]{0:T(512)S(1)}, u32[]{:S(2)}, u32[]{:S(2)}) collective-permute-start(f32[512]{0:T(512)S(1)} %get-tuple-element.76), channel_id=1, source_target_pairs={{2,0},{3,1},{4,2},{5,3},{6,4},{7,5},{8,6},{9,7},{10,8},{11,9},{12,... | collective-permute-start | bytes 6152 | tf_op jit(solution)/shard_map/ppermute | solution.py:15
  39.4 12.9 %collective-permute-start.6 = (f32[512]{0:T(512)S(1)}, f32[512]{0:T(512)S(1)}, u32[]{:S(2)}, u32[]{:S(2)}) collective-permute-start(f32[512]{0:T(512)S(1)} %get-tuple-element.75), channel_id=1, source_target_pairs={{3,0},{4,1},{5,2},{6,3},{7,4},{8,5},{9,6},{10,7},{11,8},{12,9},{13... | collective-permute-start | bytes 6152 | tf_op jit(solution)/shard_map/ppermute | solution.py:15
  40.8 0.7 copy-start.8
  41.7 10.6 copy-start.4
  41.7 10.6 collective-permute-start.7
  43.0 9.3 collective-permute-start
  47.3 5.6 collective-permute-start.1
  60.1 0.7 copy-start.6
  60.1 0.7 copy-start.7
  61.0 82.4 %copy-start.1 = (f32[125,125]{1,0:T(8,128)S(1)}, f32[125,125]{1,0:T(8,128)}, u32[]{:S(2)}) copy-start(f32[125,125]{1,0:T(8,128)} %constant.15.clone) | copy-start | bytes 187504
  236.4 27.2 %copy-start.2 = (f32[8192]{0:T(1024)S(1)}, f32[8192]{0:T(1024)}, u32[]{:S(2)}) copy-start(f32[8192]{0:T(1024)} %param.10) | copy-start | bytes 98308
  236.4 11.5 %collective-permute-start.8 = (f32[512]{0:T(512)S(1)}, f32[512]{0:T(512)S(1)}, u32[]{:S(2)}, u32[]{:S(2)}) collective-permute-start(f32[512]{0:T(512)S(1)} %get-tuple-element.55), channel_id=1, source_target_pairs={{1,0},{2,1},{3,2},{4,3},{5,4},{6,5},{7,6},{8,7},{9,8},{10,9},{11,1... | collective-permute-start | bytes 6152 | tf_op jit(solution)/shard_map/ppermute | solution.py:15
  238.4 14.5 %collective-permute-start.9 = (f32[512]{0:T(512)S(1)}, f32[512]{0:T(512)S(1)}, u32[]{:S(2)}, u32[]{:S(2)}) collective-permute-start(f32[512]{0:T(512)S(1)} %get-tuple-element.54), channel_id=1, source_target_pairs={{2,0},{3,1},{4,2},{5,3},{6,4},{7,5},{8,6},{9,7},{10,8},{11,9},{12,... | collective-permute-start | bytes 6152 | tf_op jit(solution)/shard_map/ppermute | solution.py:15
  239.7 17.8 %collective-permute-start.10 = (f32[512]{0:T(512)S(1)}, f32[512]{0:T(512)S(1)}, u32[]{:S(2)}, u32[]{:S(2)}) collective-permute-start(f32[512]{0:T(512)S(1)} %get-tuple-element.53), channel_id=1, source_target_pairs={{3,0},{4,1},{5,2},{6,3},{7,4},{8,5},{9,6},{10,7},{11,8},{12,9},{13... | collective-permute-start | bytes 6152 | tf_op jit(solution)/shard_map/ppermute | solution.py:15
  242.3 21.3 %collective-permute-start.11 = (f32[512]{0:T(512)S(1)}, f32[512]{0:T(512)S(1)}, u32[]{:S(2)}, u32[]{:S(2)}) collective-permute-start(f32[512]{0:T(512)S(1)} %get-tuple-element.52), channel_id=1, source_target_pairs={{4,0},{5,1},{6,2},{7,3},{8,4},{9,5},{10,6},{11,7},{12,8},{13,9},{1... | collective-permute-start | bytes 6152 | tf_op jit(solution)/shard_map/ppermute | solution.py:15
  243.6 20.0 %collective-permute-start.12 = (f32[512]{0:T(512)S(1)}, f32[512]{0:T(512)S(1)}, u32[]{:S(2)}, u32[]{:S(2)}) collective-permute-start(f32[512]{0:T(512)S(1)} %get-tuple-element.51), channel_id=1, source_target_pairs={{0,1},{1,2},{2,3},{3,4},{4,5},{5,6},{6,7},{7,8},{8,9},{9,10},{10,1... | collective-permute-start | bytes 6152 | tf_op jit(solution)/shard_map/ppermute | solution.py:15
  247.9 15.7 %collective-permute-start.13 = (f32[512]{0:T(512)S(1)}, f32[512]{0:T(512)S(1)}, u32[]{:S(2)}, u32[]{:S(2)}) collective-permute-start(f32[512]{0:T(512)S(1)} %get-tuple-element.50), channel_id=1, source_target_pairs={{0,2},{1,3},{2,4},{3,5},{4,6},{5,7},{6,8},{7,9},{8,10},{9,11},{10,... | collective-permute-start | bytes 6152 | tf_op jit(solution)/shard_map/ppermute | solution.py:15
  252.8 10.8 collective-permute-start.14
  257.5 6.8 collective-permute-start.15
  394.4 13.1 %collective-permute-start.16 = (f32[512]{0:T(512)S(1)}, f32[512]{0:T(512)S(1)}, u32[]{:S(2)}, u32[]{:S(2)}) collective-permute-start(f32[512]{0:T(512)S(1)} %get-tuple-element.73), channel_id=1, source_target_pairs={{0,1},{1,2},{2,3},{3,4},{4,5},{5,6},{6,7},{7,8},{8,9},{9,10},{10,1... | collective-permute-start | bytes 6152 | tf_op jit(solution)/shard_map/ppermute | solution.py:15
  396.3 12.5 %collective-permute-start.17 = (f32[512]{0:T(512)S(1)}, f32[512]{0:T(512)S(1)}, u32[]{:S(2)}, u32[]{:S(2)}) collective-permute-start(f32[512]{0:T(512)S(1)} %get-tuple-element.72), channel_id=1, source_target_pairs={{0,2},{1,3},{2,4},{3,5},{4,6},{5,7},{6,8},{7,9},{8,10},{9,11},{10,... | collective-permute-start | bytes 6152 | tf_op jit(solution)/shard_map/ppermute | solution.py:15
  398.7 11.4 %collective-permute-start.18 = (f32[512]{0:T(512)S(1)}, f32[512]{0:T(512)S(1)}, u32[]{:S(2)}, u32[]{:S(2)}) collective-permute-start(f32[512]{0:T(512)S(1)} %get-tuple-element.71), channel_id=1, source_target_pairs={{0,3},{1,4},{2,5},{3,6},{4,7},{5,8},{6,9},{7,10},{8,11},{9,12},{10... | collective-permute-start | bytes 6152 | tf_op jit(solution)/shard_map/ppermute | solution.py:15
  400.5 11.1 %collective-permute-start.19 = (f32[512]{0:T(512)S(1)}, f32[512]{0:T(512)S(1)}, u32[]{:S(2)}, u32[]{:S(2)}) collective-permute-start(f32[512]{0:T(512)S(1)} %get-tuple-element.70), channel_id=1, source_target_pairs={{0,4},{1,5},{2,6},{3,7},{4,8},{5,9},{6,10},{7,11},{8,12},{9,13},{1... | collective-permute-start | bytes 6152 | tf_op jit(solution)/shard_map/ppermute | solution.py:15
  404.9 6.7 collective-permute-start.20
  407.6 4.5 collective-permute-start.21
  408.9 6.3 collective-permute-start.22
  410.2 6.4 collective-permute-start.23
  599.1 12.2 %collective-permute-start.24 = (f32[512]{0:T(512)S(1)}, f32[512]{0:T(512)S(1)}, u32[]{:S(2)}, u32[]{:S(2)}) collective-permute-start(f32[512]{0:T(512)S(1)} %get-tuple-element.47), channel_id=1, source_target_pairs={{1,0},{2,1},{3,2},{4,3},{5,4},{6,5},{7,6},{8,7},{9,8},{10,9},{11,1... | collective-permute-start | bytes 6152 | tf_op jit(solution)/shard_map/ppermute | solution.py:15
  602.3 15.1 %collective-permute-start.25 = (f32[512]{0:T(512)S(1)}, f32[512]{0:T(512)S(1)}, u32[]{:S(2)}, u32[]{:S(2)}) collective-permute-start(f32[512]{0:T(512)S(1)} %get-tuple-element.46), channel_id=1, source_target_pairs={{2,0},{3,1},{4,2},{5,3},{6,4},{7,5},{8,6},{9,7},{10,8},{11,9},{12,... | collective-permute-start | bytes 6152 | tf_op jit(solution)/shard_map/ppermute | solution.py:15
  603.6 17.7 %collective-permute-start.26 = (f32[512]{0:T(512)S(1)}, f32[512]{0:T(512)S(1)}, u32[]{:S(2)}, u32[]{:S(2)}) collective-permute-start(f32[512]{0:T(512)S(1)} %get-tuple-element.45), channel_id=1, source_target_pairs={{3,0},{4,1},{5,2},{6,3},{7,4},{8,5},{9,6},{10,7},{11,8},{12,9},{13... | collective-permute-start | bytes 6152 | tf_op jit(solution)/shard_map/ppermute | solution.py:15
  604.9 22.3 %collective-permute-start.27 = (f32[512]{0:T(512)S(1)}, f32[512]{0:T(512)S(1)}, u32[]{:S(2)}, u32[]{:S(2)}) collective-permute-start(f32[512]{0:T(512)S(1)} %get-tuple-element.44), channel_id=1, source_target_pairs={{4,0},{5,1},{6,2},{7,3},{8,4},{9,5},{10,6},{11,7},{12,8},{13,9},{1... | collective-permute-start | bytes 6152 | tf_op jit(solution)/shard_map/ppermute | solution.py:15
  606.2 21.0 %collective-permute-start.28 = (f32[512]{0:T(512)S(1)}, f32[512]{0:T(512)S(1)}, u32[]{:S(2)}, u32[]{:S(2)}) collective-permute-start(f32[512]{0:T(512)S(1)} %get-tuple-element.43), channel_id=1, source_target_pairs={{0,1},{1,2},{2,3},{3,4},{4,5},{5,6},{6,7},{7,8},{8,9},{9,10},{10,1... | collective-permute-start | bytes 6152 | tf_op jit(solution)/shard_map/ppermute | solution.py:15
  611.3 15.8 %collective-permute-start.29 = (f32[512]{0:T(512)S(1)}, f32[512]{0:T(512)S(1)}, u32[]{:S(2)}, u32[]{:S(2)}) collective-permute-start(f32[512]{0:T(512)S(1)} %get-tuple-element.42), channel_id=1, source_target_pairs={{0,2},{1,3},{2,4},{3,5},{4,6},{5,7},{6,8},{7,9},{8,10},{9,11},{10,... | collective-permute-start | bytes 6152 | tf_op jit(solution)/shard_map/ppermute | solution.py:15
  617.4 9.7 collective-permute-start.30
  621.3 6.5 collective-permute-start.31
  750.0 12.9 %collective-permute-start.32 = (f32[512]{0:T(512)S(1)}, f32[512]{0:T(512)S(1)}, u32[]{:S(2)}, u32[]{:S(2)}) collective-permute-start(f32[512]{0:T(512)S(1)} %get-tuple-element.65), channel_id=1, source_target_pairs={{0,1},{1,2},{2,3},{3,4},{4,5},{5,6},{6,7},{7,8},{8,9},{9,10},{10,1... | collective-permute-start | bytes 6152 | tf_op jit(solution)/shard_map/ppermute | solution.py:15
  752.5 11.7 %collective-permute-start.33 = (f32[512]{0:T(512)S(1)}, f32[512]{0:T(512)S(1)}, u32[]{:S(2)}, u32[]{:S(2)}) collective-permute-start(f32[512]{0:T(512)S(1)} %get-tuple-element.64), channel_id=1, source_target_pairs={{0,2},{1,3},{2,4},{3,5},{4,6},{5,7},{6,8},{7,9},{8,10},{9,11},{10,... | collective-permute-start | bytes 6152 | tf_op jit(solution)/shard_map/ppermute | solution.py:15
  754.3 11.2 %collective-permute-start.34 = (f32[512]{0:T(512)S(1)}, f32[512]{0:T(512)S(1)}, u32[]{:S(2)}, u32[]{:S(2)}) collective-permute-start(f32[512]{0:T(512)S(1)} %get-tuple-element.63), channel_id=1, source_target_pairs={{0,3},{1,4},{2,5},{3,6},{4,7},{5,8},{6,9},{7,10},{8,11},{9,12},{10... | collective-permute-start | bytes 6152 | tf_op jit(solution)/shard_map/ppermute | solution.py:15
  756.7 10.1 collective-permute-start.35
  760.3 6.5 collective-permute-start.36
  762.9 4.5 collective-permute-start.37
  764.2 6.3 collective-permute-start.38
  765.5 6.4 collective-permute-start.39
  954.7 11.3 %collective-permute-start.40 = (f32[512]{0:T(512)S(1)}, f32[512]{0:T(512)S(1)}, u32[]{:S(2)}, u32[]{:S(2)}) collective-permute-start(f32[512]{0:T(512)S(1)} %get-tuple-element.39), channel_id=1, source_target_pairs={{1,0},{2,1},{3,2},{4,3},{5,4},{6,5},{7,6},{8,7},{9,8},{10,9},{11,1... | collective-permute-start | bytes 6152 | tf_op jit(solution)/shard_map/ppermute | solution.py:15
  957.8 14.3 %collective-permute-start.41 = (f32[512]{0:T(512)S(1)}, f32[512]{0:T(512)S(1)}, u32[]{:S(2)}, u32[]{:S(2)}) collective-permute-start(f32[512]{0:T(512)S(1)} %get-tuple-element.38), channel_id=1, source_target_pairs={{2,0},{3,1},{4,2},{5,3},{6,4},{7,5},{8,6},{9,7},{10,8},{11,9},{12,... | collective-permute-start | bytes 6152 | tf_op jit(solution)/shard_map/ppermute | solution.py:15
  959.1 16.8 %collective-permute-start.42 = (f32[512]{0:T(512)S(1)}, f32[512]{0:T(512)S(1)}, u32[]{:S(2)}, u32[]{:S(2)}) collective-permute-start(f32[512]{0:T(512)S(1)} %get-tuple-element.37), channel_id=1, source_target_pairs={{3,0},{4,1},{5,2},{6,3},{7,4},{8,5},{9,6},{10,7},{11,8},{12,9},{13... | collective-permute-start | bytes 6152 | tf_op jit(solution)/shard_map/ppermute | solution.py:15
  960.4 21.4 %collective-permute-start.43 = (f32[512]{0:T(512)S(1)}, f32[512]{0:T(512)S(1)}, u32[]{:S(2)}, u32[]{:S(2)}) collective-permute-start(f32[512]{0:T(512)S(1)} %get-tuple-element.36), channel_id=1, source_target_pairs={{4,0},{5,1},{6,2},{7,3},{8,4},{9,5},{10,6},{11,7},{12,8},{13,9},{1... | collective-permute-start | bytes 6152 | tf_op jit(solution)/shard_map/ppermute | solution.py:15
  961.7 20.1 %collective-permute-start.44 = (f32[512]{0:T(512)S(1)}, f32[512]{0:T(512)S(1)}, u32[]{:S(2)}, u32[]{:S(2)}) collective-permute-start(f32[512]{0:T(512)S(1)} %get-tuple-element.35), channel_id=1, source_target_pairs={{0,1},{1,2},{2,3},{3,4},{4,5},{5,6},{6,7},{7,8},{8,9},{9,10},{10,1... | collective-permute-start | bytes 6152 | tf_op jit(solution)/shard_map/ppermute | solution.py:15
  966.0 15.8 %collective-permute-start.45 = (f32[512]{0:T(512)S(1)}, f32[512]{0:T(512)S(1)}, u32[]{:S(2)}, u32[]{:S(2)}) collective-permute-start(f32[512]{0:T(512)S(1)} %get-tuple-element.34), channel_id=1, source_target_pairs={{0,2},{1,3},{2,4},{3,5},{4,6},{5,7},{6,8},{7,9},{8,10},{9,11},{10,... | collective-permute-start | bytes 6152 | tf_op jit(solution)/shard_map/ppermute | solution.py:15
  972.1 9.7 collective-permute-start.46
  976.0 6.5 collective-permute-start.47
